TPU v7x, 32 devices: a whole 2x2x4 slice. The times are simulated.
32 devices in a mesh: root: 4 (over z), virt: 4 (over y, x), occ: 2 (over core).
Axes of the slice: x: 2, y: 2, z: 4, core: 2. Of those that a mesh axis runs over, the one named last changes fastest.
Arguments:
- trial_singles: bfloat16 [8, 96], P('root'), may hold values from -6 to 6
- trial_doubles: bfloat16 [8, 480, 9216], P('root', 'virt', 'occ'), may hold values from -6 to 6
- occ_fock: bfloat16 [96, 96], replicated, may hold values from -0.625 to 0.625
- virt_fock: bfloat16 [480, 480], replicated, may hold values from -0.25 to 0.25
- w_ovoo: bfloat16 [96, 480, 9216], P('occ', 'virt', 'root'), may hold values from -0.625 to 0.625
- w_ooov: bfloat16 [96, 480, 9216], P('occ', 'virt', 'root'), may hold values from -0.0029296875 to 0.0029296875
- converged: int32 [8], replicated, may hold values from 0 to 1, as said below
Outputs:
- sigma_doubles: bfloat16 [8, 480, 9216], P('root', 'virt', 'occ')
- sigma_singles: float32 [8, 96], P('root')
- subspace: float32 [8, 8], P('root')
Inputs may be any that keep to these rules, and one draw needn't show every extreme that they name: `converged`: exactly 4 roots are active (0). In every draw at least one aligned block of 2 roots has all its roots active; other blocks may have none.
All inputs are finite; a program needn't handle non-finite values.
Results may differ from a plain program's by a relative error of at most 0.0044.
Values may be sent and summed in bfloat16 or wider, within the bound.
A program may use at most 256 MiB of HBM per device.

v0:
```python
import math
import jax
import jax.numpy as jnp
from jax import lax
from jax.sharding import PartitionSpec as P


def flat_pairs(left, right):
    return lax.dot_general(
        left.reshape(left.shape[0], -1),
        right.reshape(right.shape[0], -1),
        (((1,), (1,)), ((), ())),
        preferred_element_type=jnp.float32,
    )


def local(trial_singles, trial_doubles, occ_fock, virt_fock, w_ovoo, w_ooov, converged):
    local_roots, virt_local, pair_local = trial_doubles.shape
    occ_count = occ_fock.shape[0]
    virt_count = virt_fock.shape[0]
    root_count = converged.shape[0]
    root_groups = lax.axis_size("root")
    occ_groups = lax.axis_size("occ")
    root_index = lax.axis_index("root")
    occ_index = lax.axis_index("occ")
    occ_half = occ_count // occ_groups
    block_pairs = occ_count * occ_count // root_groups
    own_start = occ_index * occ_half
    active = (1 - converged).astype(jnp.float32)
    own_active = lax.dynamic_slice_in_dim(active, root_index * local_roots, local_roots)
    singles_all = lax.all_gather(trial_singles, "root", axis=0, tiled=True)
    gathered = lax.all_gather(trial_doubles, "occ", axis=2, tiled=True)
    fock_cols = lax.dynamic_slice_in_dim(occ_fock, own_start, occ_half, 1)
    batch_rows = local_roots * virt_local
    stacked = gathered.reshape(batch_rows, occ_count, occ_count)
    first_term = jnp.einsum(
        "ki,bkj->bij", fock_cols, stacked, preferred_element_type=jnp.float32
    ).reshape(local_roots, virt_local, pair_local)
    own_rows = trial_doubles.reshape(batch_rows, occ_half, occ_count)
    second_term = jnp.einsum(
        "bik,kj->bij", own_rows, occ_fock, preferred_element_type=jnp.float32
    ).reshape(local_roots, virt_local, pair_local)
    doubles_block = lax.all_to_all(gathered, "root", split_axis=2, concat_axis=0, tiled=True)
    partial_coupling = flat_pairs(doubles_block, w_ooov)
    coupling_part = lax.dynamic_update_slice(
        jnp.zeros((root_count, occ_count), jnp.float32), partial_coupling, (jnp.int32(0), own_start)
    )
    coupling = lax.psum(coupling_part, ("root", "virt", "occ"))
    singles_fock = jnp.dot(singles_all, occ_fock, preferred_element_type=jnp.float32)
    singles_every = active[:, None] * (-singles_fock - 0.5 * coupling)
    sigma_singles = lax.dynamic_slice_in_dim(singles_every, root_index * local_roots, local_roots)
    singles_cols = lax.dynamic_slice_in_dim(singles_all, own_start, occ_half, 1)
    outer_part = (
        -jnp.dot(singles_cols, w_ovoo.reshape(occ_half, -1), preferred_element_type=jnp.float32)
    ).reshape(root_count, virt_local, block_pairs)
    product = jnp.einsum(
        "ac,ncp->nap",
        virt_fock,
        lax.all_to_all(trial_doubles, "virt", split_axis=2, concat_axis=1, tiled=True),
        preferred_element_type=jnp.float32,
    ).astype(jnp.bfloat16)
    vv_term = lax.all_to_all(product, "virt", split_axis=1, concat_axis=2, tiled=True)
    vv_value = vv_term.astype(jnp.float32)
    outer_own = lax.all_to_all(outer_part, "root", split_axis=0, concat_axis=2, tiled=True)
    outer_half = lax.psum_scatter(outer_own, "occ", scatter_dimension=2, tiled=True)
    summed = vv_value + outer_half - first_term - second_term
    sigma_doubles = (own_active[:, None, None] * summed).astype(jnp.bfloat16)
    trial_piece, sigma_piece = (
        lax.all_to_all(trial_doubles, "root", split_axis=2, concat_axis=0, tiled=True),
        lax.all_to_all(sigma_doubles, "root", split_axis=2, concat_axis=0, tiled=True),
    )
    doubles_part = lax.psum(flat_pairs(trial_piece, sigma_piece), ("root", "virt", "occ"))
    singles_part = jnp.dot(
        singles_all.astype(jnp.float32), singles_every.T, precision=lax.Precision.HIGHEST
    )
    whole_matrix = doubles_part / math.sqrt(
        occ_count * occ_count * virt_count
    ) + singles_part / math.sqrt(occ_count)
    subspace = lax.dynamic_slice_in_dim(whole_matrix, root_index * local_roots, local_roots, 0)
    return (sigma_doubles, sigma_singles, subspace)


def solution(mesh):
    placed = (
        P("root", None),
        P("root", "virt", "occ"),
        P(),
        P(),
        P("occ", "virt", "root"),
        P("occ", "virt", "root"),
        P(),
    )
    return jax.shard_map(
        local,
        mesh=mesh,
        in_specs=placed,
        out_specs=(P("root", "virt", "occ"), P("root", None), P("root", None)),
        check_vma=False,
    )
```

profile of v0, /device:TPU:0, one launch (start us, length us, event | category | flops | bytes accessed | tf_op | source)
XLA Modules:
  0.0 595.7 jit_solution(10986336026013833331)
XLA Ops:
  7.2 6.9 %copy.53 = bf16[2,120,4608]{1,0,2:T(2,128)(2,1)} copy(bf16[2,120,4608]{2,1,0:T(8,128)(2,1)} %param.8) | data formatting | bytes 4423680 | tf_op args[1]
  14.1 5.2 all-to-all-start
  19.3 24.4 %copy.79 = bf16[6,8,120,2304]{3,1,2,0:T(8,128)(2,1)} copy(bf16[6,8,120,2304]{3,2,1,0:T(8,128)(2,1)} %bitcast.88) | data formatting | bytes 53084160
  43.7 11.1 %all-gather = bf16[4,2,96]{2,1,0:T(2,128)(2,1)S(1)} all-gather(bf16[1,2,96]{2,1,0:T(2,128)(2,1)S(1)} %bitcast.102), channel_id=1, replica_groups=mesh['root'=4,'virt'=4,'occ'=2] {'root'}, dimensions={0}, use_global_device_ids=true | all-gather | bytes 1920 | tf_op jit(solution)/shard_map/all_gather | solution.py:31
  54.8 10.4 %convolution_negate_fusion = f32[8,276480]{1,0:T(8,128)S(1)} fusion(bf16[48,276480]{1,0:T(8,128)(2,1)} %bitcast.84, bf16[8,96]{1,0:T(8,128)(2,1)S(1)} %bitcast.99, s32[]{:T(128)S(6)} %select_n.5), kind=kOutput, calls=%fused_computation | convolution fusion | flops 214548480 | bytes 35390980 | tf_op jit(solution)/shard_map/dot_general | solution.py:54
  65.3 6.1 %copy.57 = f32[8,120,2304]{2,1,0:T(8,128)} copy(f32[8,120,2304]{2,0,1:T(8,128)S(1)} %bitcast.85) | data formatting | bytes 17694720 | tf_op jit(solution)/shard_map/reshape | solution.py:55
  71.4 5.7 all-to-all-start.2
  77.2 0.7 all-gather.3.cloned.1.call-update
  77.8 4.4 copy.54
  82.2 2.9 fusion.4
  85.2 3.1 copy.55
  88.3 180.0 %all-to-all-done.2 = f32[8,120,2304]{2,1,0:T(8,128)} async-done(((f32[8,120,2304]{2,1,0:T(8,128)}), f32[8,120,2304]{2,1,0:T(8,128)}, u32[]{:S(2)}, u32[]{:S(2)}) %all-to-all-start.2) | async-done | bytes 8847392 | tf_op jit(solution)/shard_map/all_to_all | solution.py:64
  268.2 3.9 all-to-all-start.1
  272.1 14.5 %copy.58 = f32[2,120,4,2304]{1,0,3,2:T(2,128)} copy(f32[2,120,4,2304]{3,1,0,2:T(8,128)} %bitcast.12) | data formatting | bytes 17694720 | tf_op jit(solution)/shard_map/all_to_all | solution.py:64
  286.6 10.8 %all-to-all-done.1 = bf16[2,480,1152]{2,0,1:T(2,128)(2,1)S(1)} async-done(((bf16[2,480,1152]{2,0,1:T(2,128)(2,1)}), bf16[2,480,1152]{2,0,1:T(2,128)(2,1)S(1)}, u32[]{:S(2)}, u32[]{:S(2)}) %all-to-all-start.1) | async-done | bytes 2211872 | tf_op jit(solution)/shard_map/all_to_all | solution.py:62
  297.5 1.4 copy-done.2
  298.8 3.7 all-to-all-start.5
  302.6 12.7 %copy.65 = bf16[2,120,9216]{1,0,2:T(2,128)(2,1)} copy(bf16[2,120,9216]{2,1,0:T(8,128)(2,1)} %all-gather.3.cloned.1.call-done) | data formatting | bytes 8847360 | tf_op jit(solution)/shard_map/all_gather | solution.py:32
  315.3 40.6 %all-to-all-done.5 = bf16[2,120,4608]{1,0,2:T(2,128)(2,1)S(1)} async-done(((bf16[2,120,4608]{1,0,2:T(2,128)(2,1)}), bf16[2,120,4608]{1,0,2:T(2,128)(2,1)S(1)}, u32[]{:S(2)}, u32[]{:S(2)}) %all-to-all-start.5) | async-done | bytes 2211872 | tf_op jit(solution)/shard_map/all_to_all | solution.py:69
  356.0 5.1 all-to-all-start.3
  361.1 5.9 reshape.49
  367.0 4.7 fusion.11
  371.6 7.1 %reshape.50 = f32[2,120,4608]{1,0,2:T(2,128)} reshape(f32[240,48,96]{0,2,1:T(8,128)} %fusion.11) | data formatting | bytes 8847360 | tf_op jit(solution)/shard_map/reshape | solution.py:42
  378.9 0.6 dynamic-slice
  380.1 8.9 %copy.56 = f32[2,4,120,1152]{2,0,3,1:T(2,128)} copy(bf16[2,4,120,1152]{3,0,2,1:T(2,128)(2,1)} %bitcast.95) | data formatting | bytes 6635520 | tf_op jit(solution)/shard_map/convert_element_type | solution.py:63
  389.0 9.5 %reshape.62 = bf16[240,96,96]{2,1,0:T(8,128)(2,1)} reshape(bf16[2,120,9216]{2,1,0:T(8,128)(2,1)} %all-gather.3.cloned.1.call-done) | data formatting | bytes 8847360 | tf_op jit(solution)/shard_map/reshape | solution.py:35
  398.6 9.2 %copy.61 = bf16[240,96,96]{0,1,2:T(8,128)(2,1)} copy(bf16[240,96,96]{2,1,0:T(8,128)(2,1)} %reshape.62) | data formatting | bytes 8847360 | tf_op jit(solution)/shard_map/reshape | solution.py:35
  407.8 3.2 convolution_bitcast_fusion
  411.0 4.8 copy.62
  415.9 7.1 %reshape.48 = f32[2,120,4608]{1,0,2:T(2,128)} reshape(f32[240,48,96]{0,2,1:T(8,128)} %copy.62) | data formatting | bytes 8847360 | tf_op jit(solution)/shard_map/reshape | solution.py:38
  423.0 10.2 %fusion.3 = bf16[2,120,4608]{1,0,2:T(2,128)(2,1)} fusion(f32[2,120,4608]{1,0,2:T(2,128)} %reshape.50, f32[2,120,4608]{1,0,2:T(2,128)} %reshape.48, f32[2,120,9216]{1,0,2:T(2,128)} %all-reduce.4.cloned.1.call-done, u32[]{:T(128)S(6)} %multiply.4, f32[2,4,120,1152]{2,0,3,1:T(2,128)} %copy.56, f32[2]{0:T(128)S(1)} %dynamic_slice.15), kind=kLoop, calls=%fused_computation.5 | loop fusion | flops 5529600 | bytes 19906572 | tf_op jit(solution)/shard_map/convert_element_type | solution.py:67
  433.2 31.7 %all-to-all-done.3 = bf16[2,120,9216]{1,0,2:T(2,128)(2,1)} async-done(((bf16[2,120,9216]{1,0,2:T(2,128)(2,1)}), bf16[2,120,9216]{1,0,2:T(2,128)(2,1)}, u32[]{:S(2)}, u32[]{:S(2)}) %all-to-all-start.3) | async-done | bytes 4423712 | tf_op jit(solution)/shard_map/all_to_all | solution.py:43
  464.9 4.7 all-to-all-start.4
  469.6 24.4 %copy.81 = bf16[6,8,120,2304]{3,1,2,0:T(8,128)(2,1)} copy(bf16[6,8,120,2304]{3,2,1,0:T(8,128)(2,1)} %bitcast.89) | data formatting | bytes 53084160
  494.0 4.3 copy.69
  498.3 1.9 copy.83
  500.2 12.3 %copy.66 = bf16[2,120,4,2304]{3,1,0,2:T(8,128)(2,1)} copy(bf16[2,120,4,2304]{1,0,3,2:T(2,128)(2,1)} %bitcast.17) | data formatting | bytes 8847360 | tf_op jit(solution)/shard_map/all_to_all | solution.py:43
  512.5 5.2 copy.80
  517.7 13.4 %fusion.17 = f32[8,48]{1,0:T(8,128)S(1)} fusion(bf16[8,276480]{1,0:T(8,128)(2,1)} %bitcast.87, bf16[48,276480]{1,0:T(8,128)(2,1)} %bitcast.83), kind=kOutput, calls=%fused_computation.27 | convolution fusion | flops 212336640 | bytes 30967296 | tf_op jit(solution)/shard_map/dot_general | solution.py:9
  531.0 0.2 dynamic_update_slice.3
  531.2 6.7 %copy.71 = bf16[2,120,4608]{2,1,0:T(8,128)(2,1)} copy(bf16[2,120,4608]{1,0,2:T(2,128)(2,1)} %fusion.3) | data formatting | bytes 4423680
  537.9 6.8 %copy.67 = bf16[2,120,4,1152]{3,1,0,2:T(8,128)(2,1)} copy(bf16[2,120,4,1152]{1,0,3,2:T(2,128)(2,1)} %bitcast.19) | data formatting | bytes 4423680 | tf_op jit(solution)/shard_map/all_to_all | solution.py:70
  544.7 1.9 copy.82
  546.6 1.2 convolution_bitcast_fusion.1
  547.8 39.5 %all-reduce.1 = (f32[8,96]{1,0:T(8,128)S(1)}, f32[8,8]{0,1:T(8,128)S(1)}) all-reduce(f32[8,96]{1,0:T(8,128)S(1)} %dynamic_update_slice.3, f32[8,8]{0,1:T(8,128)S(1)} %convolution_bitcast_fusion.1), channel_id=1, replica_groups=mesh['root'=4,'virt'=4,'occ'=2] {'root','virt','occ'}, use_global_device_ids=true, to_apply=%region_1.0 | all-reduce | flops 832 | bytes 6656 | tf_op jit(solution)/shard_map/psum | solution.py:48
  587.4 0.6 constant_dynamic-slice_fusion.1
  588.0 0.1 fusion.6
  588.2 0.7 copy.72
  (25 shorter events, 0.3 us)
Async XLA Ops:
  7.2 75.1 %copy-start = (bf16[480,480]{1,0:T(8,128)(2,1)S(1)}, bf16[480,480]{1,0:T(8,128)(2,1)}, u32[]{:S(2)}) copy-start(bf16[480,480]{1,0:T(8,128)(2,1)} %param.10) | copy-start | bytes 1382404
  14.1 57.3 %all-to-all-start = ((bf16[2,120,4608]{1,0,2:T(2,128)(2,1)}), bf16[2,120,4608]{1,0,2:T(2,128)(2,1)S(1)}, u32[]{:S(2)}, u32[]{:S(2)}) async-start(bf16[2,120,4608]{1,0,2:T(2,128)(2,1)} %copy.53), calls=%async_computation | async-start | bytes 4718592 | tf_op jit(solution)/shard_map/all_to_all | solution.py:59
  19.3 24.4 %copy-start.4 = (bf16[2,96]{1,0:T(2,128)(2,1)S(1)}, bf16[2,96]{1,0:T(2,128)(2,1)}, u32[]{:S(2)}) copy-start(bf16[2,96]{1,0:T(2,128)(2,1)} %param.7) | copy-start | bytes 1156
  71.4 196.8 %all-to-all-start.2 = ((f32[8,120,2304]{2,1,0:T(8,128)}), f32[8,120,2304]{2,1,0:T(8,128)}, u32[]{:S(2)}, u32[]{:S(2)}) async-start(f32[8,120,2304]{2,1,0:T(8,128)} %copy.57), calls=%async_computation.2 | async-start | bytes 17694720 | tf_op jit(solution)/shard_map/all_to_all | solution.py:64
  77.1 225.4 %all-gather.3.cloned.1.call-start = ((), (), s32[]{:S(2)}) async-start(), calls=%async_computation.6 | async-start | bytes 6635520 | tf_op jit(solution)/shard_map/all_gather | solution.py:32
  268.2 29.2 %all-to-all-start.1 = ((bf16[2,480,1152]{2,0,1:T(2,128)(2,1)}), bf16[2,480,1152]{2,0,1:T(2,128)(2,1)S(1)}, u32[]{:S(2)}, u32[]{:S(2)}) async-start(bf16[2,480,1152]{2,0,1:T(2,128)(2,1)} %copy.55), calls=%async_computation.1 | async-start | bytes 4423680 | tf_op jit(solution)/shard_map/all_to_all | solution.py:62
  272.1 150.9 %all-reduce.4.cloned.1.call-start = ((), (), s32[]{:S(2)}) async-start(), calls=%async_computation.7 | async-start | bytes 18874368
  297.5 1.4 copy-start.2
  298.8 57.1 %all-to-all-start.5 = ((bf16[2,120,4608]{1,0,2:T(2,128)(2,1)}), bf16[2,120,4608]{1,0,2:T(2,128)(2,1)S(1)}, u32[]{:S(2)}, u32[]{:S(2)}) async-start(bf16[2,120,4608]{1,0,2:T(2,128)(2,1)} %copy.53), calls=%async_computation.5 | async-start | bytes 4718592 | tf_op jit(solution)/shard_map/all_to_all | solution.py:69
  356.0 108.9 %all-to-all-start.3 = ((bf16[2,120,9216]{1,0,2:T(2,128)(2,1)}), bf16[2,120,9216]{1,0,2:T(2,128)(2,1)}, u32[]{:S(2)}, u32[]{:S(2)}) async-start(bf16[2,120,9216]{1,0,2:T(2,128)(2,1)} %copy.65), calls=%async_computation.3 | async-start | bytes 9437184 | tf_op jit(solution)/shard_map/all_to_all | solution.py:43
  361.1 5.9 copy-start.3
  371.6 7.2 %copy-start.5 = (s32[8]{0:T(128)S(1)}, s32[8]{0:T(128)}, u32[]{:S(2)}) copy-start(s32[8]{0:T(128)} %param.13) | copy-start | bytes 100
  371.6 7.2 %copy-start.6 = (u32[32]{0:T(128)S(1)}, u32[32]{0:T(128)}, u32[]{:S(2)}) copy-start(u32[32]{0:T(128)} %constant.35) | copy-start | bytes 388
  464.9 73.0 %all-to-all-start.4 = ((bf16[2,120,4608]{1,0,2:T(2,128)(2,1)}), bf16[2,120,4608]{1,0,2:T(2,128)(2,1)}, u32[]{:S(2)}, u32[]{:S(2)}) async-start(bf16[2,120,4608]{1,0,2:T(2,128)(2,1)} %fusion.3), calls=%async_computation.4 | async-start | bytes 4718592 | tf_op jit(solution)/shard_map/all_to_all | solution.py:70
  537.9 51.0 %copy-start.1 = (bf16[480,480]{1,0:T(8,128)(2,1)S(1)}, bf16[480,480]{1,0:T(8,128)(2,1)}, u32[]{:S(2)}) copy-start(bf16[480,480]{1,0:T(8,128)(2,1)} %param.10) | copy-start | bytes 1382404
Sparse Core Ops, SparseCore 0:
  79.5 15.8 all-gather.2
  286.7 40.7 all-reduce.3
where the time goes:
time: 599 us; the launch traced here: 596 us
  waiting for transfers between devices  264 us (44%)
  local copies, waits for them, and re-layouts  192 us (32%)
  blocking collectives  50.7 us (8%)
  matrix products  36.1 us (6%)
  starting transfers between devices  28.3 us (5%)
  between operations  14.8 us (2%)
  other arithmetic  10.2 us (2%)
    all_to_all x1, waiting for transfers between devices, local(): lax.all_to_all(outer_part, 'root', split_axis=0, concat_axis=2, tiled=True)  180 us
    unnamed x23, local copies, waits for them, and re-layouts  74 us
    all_to_all x1, waiting for transfers between devices, local(): lax.all_to_all(trial_doubles, 'root', split_axis=2, concat_axis=0, tiled=...  40.6 us
    psum x1, blocking collectives, local(): coupling = lax.psum(coupling_part, ('root', 'virt', 'occ'))  39.5 us
    all_to_all x1, waiting for transfers between devices, local(): lax.all_to_all(gathered, 'root', split_axis=2, concat_axis=0, tiled=True)  31.7 us
    reshape x2, local copies, waits for them, and re-layouts, local(): stacked = gathered.reshape(batch_rows, occ_count, occ_count)  18.8 us
    dot_general x2, matrix products, flat_pairs(): lax.dot_general(left.reshape(left.shape[0], -1), right.reshape(right.shap...  14.6 us
    all_to_all x1, local copies, waits for them, and re-layouts, local(): lax.all_to_all(outer_part, 'root', split_axis=0, concat_axis=2, tiled=True)  14.5 us
  transfers between devices with their start and end apart: 8, of which 4 were waited for; matrix products, arithmetic and copies ran while one was open for 37% of the time, Pallas kernels for 0%

commit v1 on v0

--- a/solution.py
+++ b/solution.py
@@ -45,7 +45,7 @@
     coupling_part = lax.dynamic_update_slice(
         jnp.zeros((root_count, occ_count), jnp.float32), partial_coupling, (jnp.int32(0), own_start)
     )
-    coupling = lax.psum(coupling_part, ("root", "virt", "occ"))
+    coupling = lax.psum(lax.psum(coupling_part, ("virt", "occ")), "root")
     singles_fock = jnp.dot(singles_all, occ_fock, preferred_element_type=jnp.float32)
     singles_every = active[:, None] * (-singles_fock - 0.5 * coupling)
     sigma_singles = lax.dynamic_slice_in_dim(singles_every, root_index * local_roots, local_roots)

time: 599 us -> 621 us (1.037)
  blocking collectives: 50.7 us -> 71.7 us
    psum x1 -> x3, blocking collectives: 39.5 us -> 60.6 us  [the longest x1 36.8 us: local(): lax.psum(flat_pairs(trial_piece, sigma_piece), ('root', 'virt', 'occ'))]
  transfers between devices with their start and end apart: 8 -> 8, of which waited for: 4 -> 4; matrix products, arithmetic and copies ran while one was open for 37% -> 36% of each run, Pallas kernels for 0% -> 0%
where the time goes in v1:
time: 621 us; the launch traced here: 617 us
  waiting for transfers between devices  264 us (43%)
  local copies, waits for them, and re-layouts  192 us (31%)
  blocking collectives  71.7 us (12%)
  matrix products  36.1 us (6%)
  starting transfers between devices  28.4 us (5%)
  between operations  14.8 us (2%)
  other arithmetic  10.2 us (2%)
    all_to_all x1, waiting for transfers between devices, local(): lax.all_to_all(outer_part, 'root', split_axis=0, concat_axis=2, tiled=True)  180 us
    unnamed x23, local copies, waits for them, and re-layouts  74.1 us
    all_to_all x1, waiting for transfers between devices, local(): lax.all_to_all(trial_doubles, 'root', split_axis=2, concat_axis=0, tiled=...  40.7 us
    psum x1, blocking collectives, local(): lax.psum(flat_pairs(trial_piece, sigma_piece), ('root', 'virt', 'occ'))  36.8 us
    all_to_all x1, waiting for transfers between devices, local(): lax.all_to_all(gathered, 'root', split_axis=2, concat_axis=0, tiled=True)  31.6 us
    psum x2, blocking collectives, local(): coupling = lax.psum(lax.psum(coupling_part, ('virt', 'occ')), 'root')  23.8 us
    reshape x2, local copies, waits for them, and re-layouts, local(): stacked = gathered.reshape(batch_rows, occ_count, occ_count)  18.8 us
    dot_general x2, matrix products, flat_pairs(): lax.dot_general(left.reshape(left.shape[0], -1), right.reshape(right.shap...  14.6 us
  transfers between devices with their start and end apart: 8, of which 4 were waited for; matrix products, arithmetic and copies ran while one was open for 36% of the time, Pallas kernels for 0%

profile of v1, /device:TPU:0, one launch (start us, length us, event | category | flops | bytes accessed | tf_op | source)
XLA Modules:
  0.0 616.9 jit_solution(59587074410208663)
XLA Ops:
  7.2 6.9 %copy.53 = bf16[2,120,4608]{1,0,2:T(2,128)(2,1)} copy(bf16[2,120,4608]{2,1,0:T(8,128)(2,1)} %param.8) | data formatting | bytes 4423680 | tf_op args[1]
  14.1 5.2 all-to-all-start
  19.3 24.5 %copy.79 = bf16[6,8,120,2304]{3,1,2,0:T(8,128)(2,1)} copy(bf16[6,8,120,2304]{3,2,1,0:T(8,128)(2,1)} %bitcast.88) | data formatting | bytes 53084160
  43.7 11.1 %all-gather = bf16[4,2,96]{2,1,0:T(2,128)(2,1)S(1)} all-gather(bf16[1,2,96]{2,1,0:T(2,128)(2,1)S(1)} %bitcast.102), channel_id=1, replica_groups=mesh['root'=4,'virt'=4,'occ'=2] {'root'}, dimensions={0}, use_global_device_ids=true | all-gather | bytes 1920 | tf_op jit(solution)/shard_map/all_gather | solution.py:31
  54.9 10.4 %convolution_negate_fusion = f32[8,276480]{1,0:T(8,128)S(1)} fusion(bf16[48,276480]{1,0:T(8,128)(2,1)} %bitcast.84, bf16[8,96]{1,0:T(8,128)(2,1)S(1)} %bitcast.99, s32[]{:T(128)S(6)} %select_n.5), kind=kOutput, calls=%fused_computation | convolution fusion | flops 214548480 | bytes 35390980 | tf_op jit(solution)/shard_map/dot_general | solution.py:54
  65.3 6.1 copy.57
  71.5 5.7 all-to-all-start.2
  77.2 0.7 all-gather.3.cloned.1.call-update
  77.9 4.4 copy.54
  82.3 2.9 fusion.4
  85.3 3.1 copy.55
  88.3 180.0 %all-to-all-done.2 = f32[8,120,2304]{2,1,0:T(8,128)} async-done(((f32[8,120,2304]{2,1,0:T(8,128)}), f32[8,120,2304]{2,1,0:T(8,128)}, u32[]{:S(2)}, u32[]{:S(2)}) %all-to-all-start.2) | async-done | bytes 8847392 | tf_op jit(solution)/shard_map/all_to_all | solution.py:64
  268.3 3.9 all-to-all-start.1
  272.2 14.6 %copy.58 = f32[2,120,4,2304]{1,0,3,2:T(2,128)} copy(f32[2,120,4,2304]{3,1,0,2:T(8,128)} %bitcast.12) | data formatting | bytes 17694720 | tf_op jit(solution)/shard_map/all_to_all | solution.py:64
  286.8 10.8 %all-to-all-done.1 = bf16[2,480,1152]{2,0,1:T(2,128)(2,1)S(1)} async-done(((bf16[2,480,1152]{2,0,1:T(2,128)(2,1)}), bf16[2,480,1152]{2,0,1:T(2,128)(2,1)S(1)}, u32[]{:S(2)}, u32[]{:S(2)}) %all-to-all-start.1) | async-done | bytes 2211872 | tf_op jit(solution)/shard_map/all_to_all | solution.py:62
  297.6 1.4 copy-done.2
  298.9 3.7 all-to-all-start.5
  302.6 12.7 %copy.65 = bf16[2,120,9216]{1,0,2:T(2,128)(2,1)} copy(bf16[2,120,9216]{2,1,0:T(8,128)(2,1)} %all-gather.3.cloned.1.call-done) | data formatting | bytes 8847360 | tf_op jit(solution)/shard_map/all_gather | solution.py:32
  315.4 40.7 %all-to-all-done.5 = bf16[2,120,4608]{1,0,2:T(2,128)(2,1)S(1)} async-done(((bf16[2,120,4608]{1,0,2:T(2,128)(2,1)}), bf16[2,120,4608]{1,0,2:T(2,128)(2,1)S(1)}, u32[]{:S(2)}, u32[]{:S(2)}) %all-to-all-start.5) | async-done | bytes 2211872 | tf_op jit(solution)/shard_map/all_to_all | solution.py:69
  356.0 5.1 all-to-all-start.3
  361.2 5.9 reshape.49
  367.1 4.7 fusion.11
  371.8 7.2 %reshape.50 = f32[2,120,4608]{1,0,2:T(2,128)} reshape(f32[240,48,96]{0,2,1:T(8,128)} %fusion.11) | data formatting | bytes 8847360 | tf_op jit(solution)/shard_map/reshape | solution.py:42
  379.0 0.6 dynamic-slice
  380.3 8.9 %copy.56 = f32[2,4,120,1152]{2,0,3,1:T(2,128)} copy(bf16[2,4,120,1152]{3,0,2,1:T(2,128)(2,1)} %bitcast.95) | data formatting | bytes 6635520 | tf_op jit(solution)/shard_map/convert_element_type | solution.py:63
  389.2 9.5 %reshape.62 = bf16[240,96,96]{2,1,0:T(8,128)(2,1)} reshape(bf16[2,120,9216]{2,1,0:T(8,128)(2,1)} %all-gather.3.cloned.1.call-done) | data formatting | bytes 8847360 | tf_op jit(solution)/shard_map/reshape | solution.py:35
  398.7 9.3 %copy.61 = bf16[240,96,96]{0,1,2:T(8,128)(2,1)} copy(bf16[240,96,96]{2,1,0:T(8,128)(2,1)} %reshape.62) | data formatting | bytes 8847360 | tf_op jit(solution)/shard_map/reshape | solution.py:35
  408.0 3.2 convolution_bitcast_fusion
  411.2 4.8 copy.62
  416.0 7.1 %reshape.48 = f32[2,120,4608]{1,0,2:T(2,128)} reshape(f32[240,48,96]{0,2,1:T(8,128)} %copy.62) | data formatting | bytes 8847360 | tf_op jit(solution)/shard_map/reshape | solution.py:38
  423.2 10.2 %fusion.3 = bf16[2,120,4608]{1,0,2:T(2,128)(2,1)} fusion(f32[2,120,4608]{1,0,2:T(2,128)} %reshape.50, f32[2,120,4608]{1,0,2:T(2,128)} %reshape.48, f32[2,120,9216]{1,0,2:T(2,128)} %all-reduce.3.cloned.1.call-done, u32[]{:T(128)S(6)} %multiply.4, f32[2,4,120,1152]{2,0,3,1:T(2,128)} %copy.56, f32[2]{0:T(128)S(1)} %dynamic_slice.15), kind=kLoop, calls=%fused_computation.5 | loop fusion | flops 5529600 | bytes 19906572 | tf_op jit(solution)/shard_map/convert_element_type | solution.py:67
  433.4 31.6 %all-to-all-done.3 = bf16[2,120,9216]{1,0,2:T(2,128)(2,1)} async-done(((bf16[2,120,9216]{1,0,2:T(2,128)(2,1)}), bf16[2,120,9216]{1,0,2:T(2,128)(2,1)}, u32[]{:S(2)}, u32[]{:S(2)}) %all-to-all-start.3) | async-done | bytes 4423712 | tf_op jit(solution)/shard_map/all_to_all | solution.py:43
  465.0 4.7 all-to-all-start.4
  469.7 24.5 %copy.81 = bf16[6,8,120,2304]{3,1,2,0:T(8,128)(2,1)} copy(bf16[6,8,120,2304]{3,2,1,0:T(8,128)(2,1)} %bitcast.89) | data formatting | bytes 53084160
  494.2 4.3 copy.69
  498.5 1.9 copy.83
  500.4 12.2 %copy.66 = bf16[2,120,4,2304]{3,1,0,2:T(8,128)(2,1)} copy(bf16[2,120,4,2304]{1,0,3,2:T(2,128)(2,1)} %bitcast.17) | data formatting | bytes 8847360 | tf_op jit(solution)/shard_map/all_to_all | solution.py:43
  512.6 5.2 copy.80
  517.8 13.4 %fusion.17 = f32[8,48]{1,0:T(8,128)S(1)} fusion(bf16[8,276480]{1,0:T(8,128)(2,1)} %bitcast.87, bf16[48,276480]{1,0:T(8,128)(2,1)} %bitcast.83), kind=kOutput, calls=%fused_computation.27 | convolution fusion | flops 212336640 | bytes 30967296 | tf_op jit(solution)/shard_map/dot_general | solution.py:9
  531.4 11.9 %psum.21 = f32[8,96]{1,0:T(8,128)S(1)} all-reduce(f32[8,96]{1,0:T(8,128)S(1)} %dynamic_update_slice.3), channel_id=1, replica_groups=mesh['root'=4,'virt'=4,'occ'=2] {'virt','occ'}, use_global_device_ids=true, to_apply=%region_1.0 | all-reduce | flops 768 | bytes 6144 | tf_op jit(solution)/shard_map/psum | solution.py:48
  543.2 11.9 %psum.22 = f32[8,96]{1,0:T(8,128)S(1)} all-reduce(f32[8,96]{1,0:T(8,128)S(1)} %psum.21), channel_id=1, replica_groups=mesh['root'=4,'virt'=4,'occ'=2] {'root'}, use_global_device_ids=true, to_apply=%region_2.0 | all-reduce | flops 768 | bytes 6144 | tf_op jit(solution)/shard_map/psum | solution.py:48
  555.2 0.6 constant_dynamic-slice_fusion.1
  555.8 6.7 %copy.71 = bf16[2,120,4608]{2,1,0:T(8,128)(2,1)} copy(bf16[2,120,4608]{1,0,2:T(2,128)(2,1)} %fusion.3) | data formatting | bytes 4423680
  562.5 6.8 %copy.67 = bf16[2,120,4,1152]{3,1,0,2:T(8,128)(2,1)} copy(bf16[2,120,4,1152]{1,0,3,2:T(2,128)(2,1)} %bitcast.19) | data formatting | bytes 4423680 | tf_op jit(solution)/shard_map/all_to_all | solution.py:70
  569.3 1.9 copy.82
  571.2 1.2 convolution_bitcast_fusion.1
  572.4 36.8 %psum.23 = f32[8,8]{0,1:T(8,128)S(1)} all-reduce(f32[8,8]{0,1:T(8,128)S(1)} %convolution_bitcast_fusion.1), channel_id=1, replica_groups=mesh['root'=4,'virt'=4,'occ'=2] {'root','virt','occ'}, use_global_device_ids=true, to_apply=%region_3.0 | all-reduce | flops 64 | bytes 512 | tf_op jit(solution)/shard_map/psum | solution.py:72
  609.4 0.7 copy.72
  (27 shorter events, 0.6 us)
Async XLA Ops:
  7.2 75.2 %copy-start = (bf16[480,480]{1,0:T(8,128)(2,1)S(1)}, bf16[480,480]{1,0:T(8,128)(2,1)}, u32[]{:S(2)}) copy-start(bf16[480,480]{1,0:T(8,128)(2,1)} %param.10) | copy-start | bytes 1382404
  14.1 57.4 %all-to-all-start = ((bf16[2,120,4608]{1,0,2:T(2,128)(2,1)}), bf16[2,120,4608]{1,0,2:T(2,128)(2,1)S(1)}, u32[]{:S(2)}, u32[]{:S(2)}) async-start(bf16[2,120,4608]{1,0,2:T(2,128)(2,1)} %copy.53), calls=%async_computation | async-start | bytes 4718592 | tf_op jit(solution)/shard_map/all_to_all | solution.py:59
  19.3 24.5 %copy-start.4 = (bf16[2,96]{1,0:T(2,128)(2,1)S(1)}, bf16[2,96]{1,0:T(2,128)(2,1)}, u32[]{:S(2)}) copy-start(bf16[2,96]{1,0:T(2,128)(2,1)} %param.7) | copy-start | bytes 1156
  71.5 196.8 %all-to-all-start.2 = ((f32[8,120,2304]{2,1,0:T(8,128)}), f32[8,120,2304]{2,1,0:T(8,128)}, u32[]{:S(2)}, u32[]{:S(2)}) async-start(f32[8,120,2304]{2,1,0:T(8,128)} %copy.57), calls=%async_computation.2 | async-start | bytes 17694720 | tf_op jit(solution)/shard_map/all_to_all | solution.py:64
  77.2 225.4 %all-gather.3.cloned.1.call-start = ((), (), s32[]{:S(2)}) async-start(), calls=%async_computation.6 | async-start | bytes 6635520 | tf_op jit(solution)/shard_map/all_gather | solution.py:32
  268.3 29.2 %all-to-all-start.1 = ((bf16[2,480,1152]{2,0,1:T(2,128)(2,1)}), bf16[2,480,1152]{2,0,1:T(2,128)(2,1)S(1)}, u32[]{:S(2)}, u32[]{:S(2)}) async-start(bf16[2,480,1152]{2,0,1:T(2,128)(2,1)} %copy.55), calls=%async_computation.1 | async-start | bytes 4423680 | tf_op jit(solution)/shard_map/all_to_all | solution.py:62
  272.2 151.0 %all-reduce.3.cloned.1.call-start = ((), (), s32[]{:S(2)}) async-start(), calls=%async_computation.7 | async-start | bytes 18874368
  297.6 1.4 copy-start.2
  298.9 57.1 %all-to-all-start.5 = ((bf16[2,120,4608]{1,0,2:T(2,128)(2,1)}), bf16[2,120,4608]{1,0,2:T(2,128)(2,1)S(1)}, u32[]{:S(2)}, u32[]{:S(2)}) async-start(bf16[2,120,4608]{1,0,2:T(2,128)(2,1)} %copy.53), calls=%async_computation.5 | async-start | bytes 4718592 | tf_op jit(solution)/shard_map/all_to_all | solution.py:69
  356.0 108.9 %all-to-all-start.3 = ((bf16[2,120,9216]{1,0,2:T(2,128)(2,1)}), bf16[2,120,9216]{1,0,2:T(2,128)(2,1)}, u32[]{:S(2)}, u32[]{:S(2)}) async-start(bf16[2,120,9216]{1,0,2:T(2,128)(2,1)} %copy.65), calls=%async_computation.3 | async-start | bytes 9437184 | tf_op jit(solution)/shard_map/all_to_all | solution.py:43
  361.2 5.9 copy-start.3
  371.8 7.2 %copy-start.5 = (s32[8]{0:T(128)S(1)}, s32[8]{0:T(128)}, u32[]{:S(2)}) copy-start(s32[8]{0:T(128)} %param.13) | copy-start | bytes 100
  371.8 7.3 %copy-start.6 = (u32[32]{0:T(128)S(1)}, u32[32]{0:T(128)}, u32[]{:S(2)}) copy-start(u32[32]{0:T(128)} %constant.35) | copy-start | bytes 388
  465.0 97.5 %all-to-all-start.4 = ((bf16[2,120,4608]{1,0,2:T(2,128)(2,1)}), bf16[2,120,4608]{1,0,2:T(2,128)(2,1)}, u32[]{:S(2)}, u32[]{:S(2)}) async-start(bf16[2,120,4608]{1,0,2:T(2,128)(2,1)} %fusion.3), calls=%async_computation.4 | async-start | bytes 4718592 | tf_op jit(solution)/shard_map/all_to_all | solution.py:70
  562.5 47.6 %copy-start.1 = (bf16[480,480]{1,0:T(8,128)(2,1)S(1)}, bf16[480,480]{1,0:T(8,128)(2,1)}, u32[]{:S(2)}) copy-start(bf16[480,480]{1,0:T(8,128)(2,1)} %param.10) | copy-start | bytes 1382404
Sparse Core Ops, SparseCore 0:
  79.5 15.8 all-gather.2
  286.9 40.7 all-reduce.2
